TPU v7x, 32 devices: a whole 2x2x4 slice. The times are simulated.
32 devices in a mesh: pipe: 4 (over z), row: 4 (over x, core), col: 2 (over y).
Axes of the slice: x: 2, y: 2, z: 4, core: 2. Of those that a mesh axis runs over, the one named last changes fastest.
Arguments:
- weights: bfloat16 [4, 4096, 14336], P('pipe', 'col', 'row'), may hold values from -0.09375 to 0.09375
- fwd_resid: bfloat16 [4, 128, 4096], P('pipe', None, 'col'), may hold values from -6 to 6
- fwd_hidden: bfloat16 [4, 128, 14336], P('pipe', None, 'row'), may hold values from -6 to 6
- bwd_resid: bfloat16 [4, 128, 4096], P('pipe', None, 'col'), may hold values from -6 to 6
- bwd_hidden: bfloat16 [4, 128, 14336], P('pipe', None, 'row'), may hold values from -6 to 6
- saved_pre: bfloat16 [4, 4, 128, 14336], P(None, 'pipe', None, 'row'), may hold values from -6 to 6
- pool_embed: bfloat16 [3, 128, 4096], P(None, None, 'col'), may hold values from -6 to 6
- pool_mask: int32 [3, 128], replicated, may hold values 0 or 1
- pool_stratum: int32 [3], replicated, may hold values from 0 to 7
- order: int32 [3], replicated, may hold values from 0 to 2, each once
- mask_vec: bfloat16 [4096], P('col'), may hold values from -6 to 6
- ratio_table: bfloat16 [8, 4096], P(None, 'col'), may hold values from -6 to 6
- cot_inject: bfloat16 [3, 128, 4096], P(None, None, 'col'), may hold values from -6 to 6
Outputs:
- out_resid: bfloat16 [2, 4, 128, 4096], P(None, 'pipe', None, 'col')
- out_hidden: bfloat16 [4, 128, 14336], P('pipe', 'col', 'row')
Inputs may be any that keep to these rules, and one draw needn't show every extreme that they name: `order`: each waiting micro-batch enters exactly once.
All inputs are finite; a program needn't handle non-finite values.
Results may differ from a plain program's by a relative error of at most 0.025.
Values may be sent and summed in bfloat16 or wider, within the bound.
No kernel may reach another device: no remote copies, remote signals or barrier semaphores. Data moves between devices by JAX's collectives and lax.ppermute only.
A program may use at most 64 MiB of HBM per device.

v0:
```python
import jax
import jax.numpy as jnp
from jax import lax
from jax.sharding import PartitionSpec as P

STEPS = 4


def extended_2(shard, sides, width):
    for axis, dim in sides:
        size, length = (lax.axis_size(axis), shard.shape[dim])
        up = [(i, (i + 1) % size) for i in range(size - 1)]
        down = [(j, i) for i, j in up]
        last = lax.slice_in_dim(shard, length - width, length, axis=dim)
        first = lax.slice_in_dim(shard, 0, width, axis=dim)
        before = lax.ppermute(last, axis, up)
        after = lax.ppermute(first, axis, down)
        shard = jnp.concatenate([before, shard, after], axis=dim)
    return shard


def swapped(value, axis, stride):
    mask = 2**stride
    pairs = [(source, source ^ mask) for source in range(lax.axis_size(axis))]
    return lax.ppermute(value, axis, pairs)


def silu_grad(preact):
    sigma = jax.nn.sigmoid(preact)
    return sigma * (1.0 + preact * (1.0 - sigma))


def inject(step_idx, pool_embed, pool_mask, pool_stratum, order, mask_vec, ratio_table):
    chosen = order[step_idx - 1]
    embedded = pool_embed[chosen]
    masked = pool_mask[chosen]
    stratum = pool_stratum[chosen]
    onehot = (jnp.arange(ratio_table.shape[0], dtype=jnp.int32) == stratum).astype(jnp.bfloat16)
    condition = jnp.dot(onehot, ratio_table, preferred_element_type=jnp.float32)
    chosen_rows = jnp.where(
        masked[:, None] == 1, mask_vec[None, :].astype(jnp.float32), embedded.astype(jnp.float32)
    )
    return (chosen_rows + condition[None, :]).astype(jnp.bfloat16)


def shards(
    weights,
    fwd_resid,
    fwd_hidden,
    bwd_resid,
    bwd_hidden,
    saved_pre,
    pool_embed,
    pool_mask,
    pool_stratum,
    order,
    mask_vec,
    ratio_table,
    cot_inject,
):
    weight = weights[0]
    fwd_res = fwd_resid[0]
    fwd_hid = fwd_hidden[0]
    bwd_res = bwd_resid[0]
    bwd_hid = bwd_hidden[0]
    position = lax.axis_index("pipe")
    sections = lax.axis_size("pipe")
    is_even = position % 2 == 0
    token_rows = fwd_res.shape[0]
    col_rows = token_rows // lax.axis_size("col")
    fwd_out, bwd_out, hid_share = (fwd_res, bwd_res, fwd_hid)
    for step_idx in range(STEPS):
        operand = jnp.where(is_even, fwd_res, bwd_res)

        def feature_term(offset, length, operand=operand):
            return jnp.dot(operand, weight, preferred_element_type=jnp.float32)

        preact = lax.psum_scatter(
            feature_term(jnp.int32(0), col_rows * lax.axis_size("col")).astype(jnp.bfloat16),
            "col",
            scatter_dimension=0,
            tiled=True,
        ).astype(jnp.float32)
        hid_share = jnp.where(is_even, jax.nn.silu(preact), preact).astype(jnp.bfloat16)
        hid_grad = (
            bwd_hid.astype(jnp.float32) * silu_grad(saved_pre[step_idx, 0].astype(jnp.float32))
        ).astype(jnp.bfloat16)
        hid_operand = jnp.where(is_even, hid_grad, fwd_hid)
        residual = jnp.where(is_even, bwd_res, fwd_res)
        product = lax.dot_general(
            hid_operand, weight, (((1,), (1,)), ((), ())), preferred_element_type=jnp.float32
        )
        updated = (
            residual.astype(jnp.float32)
            + lax.psum(product.astype(jnp.bfloat16), "row").astype(jnp.float32)
        ).astype(jnp.bfloat16)
        fwd_out = jnp.where(is_even, fwd_res, updated)
        bwd_out = jnp.where(is_even, updated, bwd_res)
        if step_idx + 1 < STEPS:
            hid_send = lax.all_gather(hid_share, "col", axis=0, tiled=True)
            res_rows = fwd_out.size // 128
            buffer = jnp.concatenate(
                [bwd_out.reshape(res_rows, 128), fwd_out.reshape(res_rows, 128)], 0
            )
            extended = extended_2(buffer, (("pipe", 0),), res_rows)
            left_resid = extended[:res_rows]
            right_resid = extended[extended.shape[0] - res_rows :]
            partner_hidden = swapped(hid_send, "pipe", 0)
            fwd_hid = partner_hidden
            bwd_hid = partner_hidden
            incoming = inject(
                step_idx + 1, pool_embed, pool_mask, pool_stratum, order, mask_vec, ratio_table
            )
            fwd_res = jnp.where(position == 0, incoming, left_resid.reshape(fwd_out.shape))
            bwd_res = jnp.where(
                position == sections - 1, cot_inject[step_idx], right_resid.reshape(bwd_out.shape)
            )
    out_resid = jnp.stack([fwd_out, bwd_out])[:, None]
    return (out_resid, hid_share[None])


def solution(mesh):
    return jax.shard_map(
        shards,
        mesh=mesh,
        in_specs=(
            P("pipe", "col", "row"),
            P("pipe", None, "col"),
            P("pipe", None, "row"),
            P("pipe", None, "col"),
            P("pipe", None, "row"),
            P(None, "pipe", None, "row"),
            P(None, None, "col"),
            P(),
            P(),
            P(),
            P("col"),
            P(None, "col"),
            P(None, None, "col"),
        ),
        out_specs=(P(None, "pipe", None, "col"), P("pipe", "col", "row")),
        check_vma=False,
    )
```

profile of v0, /device:TPU:0, one launch (start us, length us, event | category | flops | bytes accessed | tf_op | source)
XLA Modules:
  0.0 378.4 jit_solution(14535607205255028792)
XLA Ops:
  7.2 8.4 %fusion.16 = bf16[128,3584]{1,0:T(8,128)(2,1)} fusion(bf16[1,2048,3584]{2,1,0:T(8,128)(2,1)} %param.13, bf16[1,128,2048]{2,1,0:T(8,128)(2,1)} %param.14, bf16[1,128,2048]{2,1,0:T(8,128)(2,1)} %param.16, pred[]{:T(512)S(6)} %eq.66), kind=kOutput, calls=%fused_computation.16 | convolution fusion | flops 1879769088 | bytes 16646145 | tf_op jit(solution)/shard_map/dot_general | solution.py:76
  15.7 21.8 %reduce-scatter.5.cloned.1.call-done = bf16[64,3584]{1,0:T(8,128)(2,1)} async-done(((bf16[128,3584]{1,0:T(8,128)(2,1)}), bf16[64,3584]{1,0:T(8,128)(2,1)}) %reduce-scatter.5.cloned.1.call-update) | async-done | bytes 458768 | tf_op jit(solution)/shard_map/reduce_scatter | solution.py:78
  38.8 12.7 %all_gather.9 = bf16[128,3584]{1,0:T(8,128)(2,1)S(1)} all-gather(bf16[64,3584]{1,0:T(8,128)(2,1)S(1)} %fusion.98), channel_id=1, replica_groups=mesh['pipe'=4,'row'=4,'col'=2] {'col'}, dimensions={0}, use_global_device_ids=true | all-gather | bytes 1376256 | tf_op jit(solution)/shard_map/all_gather | solution.py:100
  53.0 11.1 %fusion.28 = bf16[128,2048]{1,0:T(8,128)(2,1)} fusion(bf16[1,2048,3584]{2,1,0:T(8,128)(2,1)} %param.13, bf16[1,128,3584]{2,1,0:T(8,128)(2,1)S(1)} %copy-done.8, bf16[1,128,3584]{2,1,0:T(8,128)(2,1)S(1)} %copy-done.9, bf16[4,1,128,3584]{3,2,1,0:T(8,128)(2,1)} %param.18, pred[]{:T(512)S(6)} %eq.66), kind=kOutput, calls=%fused_computation.20 | convolution fusion | flops 1884815360 | bytes 17956864 | tf_op jit(solution)/shard_map/dot_general | solution.py:90
  64.1 8.4 %collective-permute-done.2 = bf16[128,3584]{1,0:T(8,128)(2,1)S(1)} collective-permute-done((bf16[128,3584]{1,0:T(8,128)(2,1)S(1)}, bf16[128,3584]{1,0:T(8,128)(2,1)S(1)}, u32[]{:S(2)}, u32[]{:S(2)}) %collective-permute-start.2) | collective-permute-done | bytes 917536 | tf_op jit(solution)/shard_map/ppermute | solution.py:25
  72.6 11.1 %fusion.31 = bf16[128,2048]{1,0:T(8,128)(2,1)} fusion(bf16[1,2048,3584]{2,1,0:T(8,128)(2,1)} %param.13, bf16[128,3584]{1,0:T(8,128)(2,1)S(1)} %collective-permute-done.2, bf16[4,1,128,3584]{3,2,1,0:T(8,128)(2,1)} %param.18, pred[]{:T(512)S(6)} %eq.66), kind=kOutput, calls=%fused_computation.21 | convolution fusion | flops 1884815360 | bytes 17039360 | tf_op jit(solution)/shard_map/dot_general | solution.py:90
  92.0 28.2 %all-reduce.7.cloned.1.call-done = (bf16[128,2048]{1,0:T(8,128)(2,1)}, bf16[128,2048]{1,0:T(8,128)(2,1)}) async-done(((bf16[128,2048]{1,0:T(8,128)(2,1)}, bf16[128,2048]{1,0:T(8,128)(2,1)}), (bf16[128,2048]{1,0:T(8,128)(2,1)}, bf16[128,2048]{1,0:T(8,128)(2,1)})) %all-reduce.7.cloned.1.call-update) | async-done | bytes 1048592 | tf_op jit(solution)/shard_map/psum | solution.py:95
  124.9 4.2 %collective-permute-start = (bf16[2048,128]{1,0:T(8,128)(2,1)}, bf16[2048,128]{1,0:T(8,128)(2,1)}, u32[]{:S(2)}, u32[]{:S(2)}) collective-permute-start(bf16[2048,128]{1,0:T(8,128)(2,1)} %reshape.152), channel_id=1, source_target_pairs={{0,8},{8,16},{16,24},{1,9},{9,17},{17,25},{2,10},{10,18},{18,26},{... | collective-permute-start | bytes 1572872 | tf_op jit(solution)/shard_map/ppermute | solution.py:16
  141.2 4.9 %collective-permute-done.1 = bf16[2048,128]{1,0:T(8,128)(2,1)} collective-permute-done((bf16[2048,128]{1,0:T(8,128)(2,1)}, bf16[2048,128]{1,0:T(8,128)(2,1)}, u32[]{:S(2)}, u32[]{:S(2)}) %collective-permute-start.1) | collective-permute-done | bytes 524320 | tf_op jit(solution)/shard_map/ppermute | solution.py:17
  166.2 6.4 %collective-permute-done.4 = bf16[2048,128]{1,0:T(8,128)(2,1)} collective-permute-done((bf16[2048,128]{1,0:T(8,128)(2,1)}, bf16[2048,128]{1,0:T(8,128)(2,1)}, u32[]{:S(2)}, u32[]{:S(2)}) %collective-permute-start.4) | collective-permute-done | bytes 524320 | tf_op jit(solution)/shard_map/ppermute | solution.py:17
  177.7 8.4 %fusion.19 = bf16[128,3584]{1,0:T(8,128)(2,1)} fusion(bf16[128,2048]{1,0:T(8,128)(2,1)} %select_n.258, bf16[1,2048,3584]{2,1,0:T(8,128)(2,1)} %param.13), kind=kOutput, calls=%fused_computation.17 | convolution fusion | flops 1879506944 | bytes 16121856 | tf_op jit(solution)/shard_map/dot_general | solution.py:76
  188.2 8.7 %fusion.22 = bf16[128,3584]{1,0:T(8,128)(2,1)} fusion(bf16[128,2048]{1,0:T(8,128)(2,1)} %select_n.270, bf16[1,2048,3584]{2,1,0:T(8,128)(2,1)} %param.13), kind=kOutput, calls=%fused_computation.18 | convolution fusion | flops 1879506944 | bytes 16121856 | tf_op jit(solution)/shard_map/dot_general | solution.py:76
  196.9 7.1 %reduce-scatter.7.cloned.1.call-done = bf16[64,3584]{1,0:T(8,128)(2,1)} async-done(((bf16[128,3584]{1,0:T(8,128)(2,1)}), bf16[64,3584]{1,0:T(8,128)(2,1)}) %reduce-scatter.7.cloned.1.call-update) | async-done | bytes 458768 | tf_op jit(solution)/shard_map/reduce_scatter | solution.py:78
  205.3 18.1 %all_gather.10 = bf16[128,3584]{1,0:T(8,128)(2,1)} all-gather(bf16[64,3584]{1,0:T(8,128)(2,1)S(1)} %fusion.99), channel_id=1, replica_groups=mesh['pipe'=4,'row'=4,'col'=2] {'col'}, dimensions={0}, use_global_device_ids=true | all-gather | bytes 1376256 | tf_op jit(solution)/shard_map/all_gather | solution.py:100
  224.9 4.2 %reduce-scatter.9.cloned.1.call-done = bf16[64,3584]{1,0:T(8,128)(2,1)} async-done(((bf16[128,3584]{1,0:T(8,128)(2,1)}), bf16[64,3584]{1,0:T(8,128)(2,1)}) %reduce-scatter.9.cloned.1.call-update) | async-done | bytes 458768 | tf_op jit(solution)/shard_map/reduce_scatter | solution.py:78
  230.4 13.0 %all_gather.11 = bf16[128,3584]{1,0:T(8,128)(2,1)S(1)} all-gather(bf16[64,3584]{1,0:T(8,128)(2,1)S(1)} %fusion.100), channel_id=1, replica_groups=mesh['pipe'=4,'row'=4,'col'=2] {'col'}, dimensions={0}, use_global_device_ids=true | all-gather | bytes 1376256 | tf_op jit(solution)/shard_map/all_gather | solution.py:100
  244.9 11.7 %fusion.34 = bf16[128,2048]{1,0:T(8,128)(2,1)} fusion(bf16[1,2048,3584]{2,1,0:T(8,128)(2,1)} %param.13, bf16[128,3584]{1,0:T(8,128)(2,1)} %collective-permute-done.5, bf16[4,1,128,3584]{3,2,1,0:T(8,128)(2,1)} %param.18, pred[]{:T(512)S(6)} %eq.66), kind=kOutput, calls=%fused_computation.22 | convolution fusion | flops 1884815360 | bytes 17039360 | tf_op jit(solution)/shard_map/dot_general | solution.py:90
  256.5 8.2 %collective-permute-done.8 = bf16[128,3584]{1,0:T(8,128)(2,1)S(1)} collective-permute-done((bf16[128,3584]{1,0:T(8,128)(2,1)S(1)}, bf16[128,3584]{1,0:T(8,128)(2,1)S(1)}, u32[]{:S(2)}, u32[]{:S(2)}) %collective-permute-start.8) | collective-permute-done | bytes 917536 | tf_op jit(solution)/shard_map/ppermute | solution.py:25
  264.8 11.0 %fusion.37 = bf16[128,2048]{1,0:T(8,128)(2,1)} fusion(bf16[1,2048,3584]{2,1,0:T(8,128)(2,1)} %param.13, bf16[128,3584]{1,0:T(8,128)(2,1)S(1)} %collective-permute-done.8, bf16[4,1,128,3584]{3,2,1,0:T(8,128)(2,1)} %param.18, pred[]{:T(512)S(6)} %eq.66), kind=kOutput, calls=%fused_computation.23 | convolution fusion | flops 1884815360 | bytes 17039360 | tf_op jit(solution)/shard_map/dot_general | solution.py:90
  280.2 32.1 %all-reduce.5.cloned.1.call-done = (bf16[128,2048]{1,0:T(8,128)(2,1)}, bf16[128,2048]{1,0:T(8,128)(2,1)}) async-done(((bf16[128,2048]{1,0:T(8,128)(2,1)}, bf16[128,2048]{1,0:T(8,128)(2,1)}), (bf16[128,2048]{1,0:T(8,128)(2,1)}, bf16[128,2048]{1,0:T(8,128)(2,1)})) %all-reduce.5.cloned.1.call-update) | async-done | bytes 1048592 | tf_op jit(solution)/shard_map/psum | solution.py:95
  317.1 4.3 %collective-permute-start.6 = (bf16[2048,128]{1,0:T(8,128)(2,1)}, bf16[2048,128]{1,0:T(8,128)(2,1)}, u32[]{:S(2)}, u32[]{:S(2)}) collective-permute-start(bf16[2048,128]{1,0:T(8,128)(2,1)} %reshape.160), channel_id=1, source_target_pairs={{0,8},{8,16},{16,24},{1,9},{9,17},{17,25},{2,10},{10,18},{18,26},{... | collective-permute-start | bytes 1572872 | tf_op jit(solution)/shard_map/ppermute | solution.py:16
  331.6 7.0 %collective-permute-done.7 = bf16[2048,128]{1,0:T(8,128)(2,1)} collective-permute-done((bf16[2048,128]{1,0:T(8,128)(2,1)}, bf16[2048,128]{1,0:T(8,128)(2,1)}, u32[]{:S(2)}, u32[]{:S(2)}) %collective-permute-start.7) | collective-permute-done | bytes 524320 | tf_op jit(solution)/shard_map/ppermute | solution.py:17
  342.9 8.4 %fusion.25 = bf16[128,3584]{1,0:T(8,128)(2,1)} fusion(bf16[128,2048]{1,0:T(8,128)(2,1)} %select_n.279, bf16[1,2048,3584]{2,1,0:T(8,128)(2,1)} %param.13), kind=kOutput, calls=%fused_computation.19 | convolution fusion | flops 1879506944 | bytes 16121856 | tf_op jit(solution)/shard_map/dot_general | solution.py:76
  358.3 11.2 %reduce-scatter.11.cloned.1.call-done = bf16[64,3584]{1,0:T(8,128)(2,1)} async-done(((bf16[128,3584]{1,0:T(8,128)(2,1)}), bf16[64,3584]{1,0:T(8,128)(2,1)}) %reduce-scatter.11.cloned.1.call-update) | async-done | bytes 458768 | tf_op jit(solution)/shard_map/reduce_scatter | solution.py:78
  (90 shorter events, 87.7 us)
Async XLA Ops:
  7.2 130.0 %copy-start = (bf16[8,2048]{1,0:T(8,128)(2,1)S(1)}, bf16[8,2048]{1,0:T(8,128)(2,1)}, u32[]{:S(2)}) copy-start(bf16[8,2048]{1,0:T(8,128)(2,1)} %param.24) | copy-start | bytes 98308
  7.2 30.3 %reduce-scatter.5.cloned.1.call-start = ((), (), s32[]{:S(2)}) async-start(), calls=%async_computation.4 | async-start | bytes 1376256 | tf_op jit(solution)/shard_map/reduce_scatter | solution.py:78
  15.6 37.4 %copy-start.8 = (bf16[1,128,3584]{2,1,0:T(8,128)(2,1)S(1)}, bf16[1,128,3584]{2,1,0:T(8,128)(2,1)}, u32[]{:S(2)}) copy-start(bf16[1,128,3584]{2,1,0:T(8,128)(2,1)} %param.15) | copy-start | bytes 2752516
  15.6 37.4 %copy-start.9 = (bf16[1,128,3584]{2,1,0:T(8,128)(2,1)S(1)}, bf16[1,128,3584]{2,1,0:T(8,128)(2,1)}, u32[]{:S(2)}) copy-start(bf16[1,128,3584]{2,1,0:T(8,128)(2,1)} %param.17) | copy-start | bytes 2752516
  15.6 104.6 %all-reduce.7.cloned.1.call-start = ((), (), s32[]{:S(2)}) async-start(), calls=%async_computation.9 | async-start | bytes 2097152 | tf_op jit(solution)/shard_map/psum | solution.py:95
  51.5 21.0 %collective-permute-start.2 = (bf16[128,3584]{1,0:T(8,128)(2,1)S(1)}, bf16[128,3584]{1,0:T(8,128)(2,1)S(1)}, u32[]{:S(2)}, u32[]{:S(2)}) collective-permute-start(bf16[128,3584]{1,0:T(8,128)(2,1)S(1)} %all_gather.9), channel_id=1, source_target_pairs={{0,8},{8,0},{16,24},{24,16},{1,9},{9,1},{17,25},{25,17},{2,10},{10... | collective-permute-start | bytes 2752520 | tf_op jit(solution)/shard_map/ppermute | solution.py:25
  64.1 19.6 %copy-start.4 = (s32[3]{0:T(128)S(1)}, s32[3]{0:T(128)}, u32[]{:S(2)}) copy-start(s32[3]{0:T(128)} %param.22) | copy-start | bytes 40
  72.5 17.7 %copy-start.1 = (bf16[3,128,2048]{2,1,0:T(8,128)(2,1)S(1)}, bf16[3,128,2048]{2,1,0:T(8,128)(2,1)}, u32[]{:S(2)}) copy-start(bf16[3,128,2048]{2,1,0:T(8,128)(2,1)} %param.19) | copy-start | bytes 4718596
  83.7 120.3 %reduce-scatter.7.cloned.1.call-start = ((), (), s32[]{:S(2)}) async-start(), calls=%async_computation.5 | async-start | bytes 1376256 | tf_op jit(solution)/shard_map/reduce_scatter | solution.py:78
  90.2 30.0 %copy-start.3 = (bf16[1,128,2048]{2,1,0:T(8,128)(2,1)S(1)}, bf16[1,128,2048]{2,1,0:T(8,128)(2,1)}, u32[]{:S(2)}) copy-start(bf16[1,128,2048]{2,1,0:T(8,128)(2,1)} %param.14) | copy-start | bytes 1572868
  120.2 12.2 %copy-start.7 = (s32[3,128]{1,0:T(4,128)S(1)}, s32[3,128]{1,0:T(4,128)}, u32[]{:S(2)}) copy-start(s32[3,128]{1,0:T(4,128)} %param.20) | copy-start | bytes 4612
  124.9 14.3 %collective-permute-start = (bf16[2048,128]{1,0:T(8,128)(2,1)}, bf16[2048,128]{1,0:T(8,128)(2,1)}, u32[]{:S(2)}, u32[]{:S(2)}) collective-permute-start(bf16[2048,128]{1,0:T(8,128)(2,1)} %reshape.152), channel_id=1, source_target_pairs={{0,8},{8,16},{16,24},{1,9},{9,17},{17,25},{2,10},{10,18},{18,26},{... | collective-permute-start | bytes 1572872 | tf_op jit(solution)/shard_map/ppermute | solution.py:16
  131.1 15.0 %collective-permute-start.1 = (bf16[2048,128]{1,0:T(8,128)(2,1)}, bf16[2048,128]{1,0:T(8,128)(2,1)}, u32[]{:S(2)}, u32[]{:S(2)}) collective-permute-start(bf16[2048,128]{1,0:T(8,128)(2,1)} %reshape.154), channel_id=1, source_target_pairs={{8,0},{16,8},{24,16},{9,1},{17,9},{25,17},{10,2},{18,10},{26,18},{... | collective-permute-start | bytes 1572872 | tf_op jit(solution)/shard_map/ppermute | solution.py:17
  132.8 4.3 %copy-start.6 = (bf16[2048]{0:T(1024)(128)(2,1)S(1)}, bf16[2048]{0:T(1024)(128)(2,1)}, u32[]{:S(2)}) copy-start(bf16[2048]{0:T(1024)(128)(2,1)} %param.23) | copy-start | bytes 12292
  134.0 14.2 %copy-start.2 = (bf16[3,128,2048]{2,1,0:T(8,128)(2,1)S(1)}, bf16[3,128,2048]{2,1,0:T(8,128)(2,1)}, u32[]{:S(2)}) copy-start(bf16[3,128,2048]{2,1,0:T(8,128)(2,1)} %param.25) | copy-start | bytes 4718596
  153.0 13.2 %collective-permute-start.3 = (bf16[2048,128]{1,0:T(8,128)(2,1)}, bf16[2048,128]{1,0:T(8,128)(2,1)}, u32[]{:S(2)}, u32[]{:S(2)}) collective-permute-start(bf16[2048,128]{1,0:T(8,128)(2,1)} %reshape.156), channel_id=1, source_target_pairs={{0,8},{8,16},{16,24},{1,9},{9,17},{17,25},{2,10},{10,18},{18,26},{... | collective-permute-start | bytes 1572872 | tf_op jit(solution)/shard_map/ppermute | solution.py:16
  158.7 13.9 %collective-permute-start.4 = (bf16[2048,128]{1,0:T(8,128)(2,1)}, bf16[2048,128]{1,0:T(8,128)(2,1)}, u32[]{:S(2)}, u32[]{:S(2)}) collective-permute-start(bf16[2048,128]{1,0:T(8,128)(2,1)} %reshape.158), channel_id=1, source_target_pairs={{8,0},{16,8},{24,16},{9,1},{17,9},{25,17},{10,2},{18,10},{26,18},{... | collective-permute-start | bytes 1572872 | tf_op jit(solution)/shard_map/ppermute | solution.py:17
  186.1 43.0 %reduce-scatter.9.cloned.1.call-start = ((), (), s32[]{:S(2)}) async-start(), calls=%async_computation.6 | async-start | bytes 1376256 | tf_op jit(solution)/shard_map/reduce_scatter | solution.py:78
  196.9 115.4 %all-reduce.5.cloned.1.call-start = ((), (), s32[]{:S(2)}) async-start(), calls=%async_computation.8 | async-start | bytes 2097152 | tf_op jit(solution)/shard_map/psum | solution.py:95
  223.4 21.5 %collective-permute-start.5 = (bf16[128,3584]{1,0:T(8,128)(2,1)}, bf16[128,3584]{1,0:T(8,128)(2,1)}, u32[]{:S(2)}, u32[]{:S(2)}) collective-permute-start(bf16[128,3584]{1,0:T(8,128)(2,1)} %all_gather.10), channel_id=1, source_target_pairs={{0,8},{8,0},{16,24},{24,16},{1,9},{9,1},{17,25},{25,17},{2,10},{10... | collective-permute-start | bytes 2752520 | tf_op jit(solution)/shard_map/ppermute | solution.py:25
  243.4 21.4 %collective-permute-start.8 = (bf16[128,3584]{1,0:T(8,128)(2,1)S(1)}, bf16[128,3584]{1,0:T(8,128)(2,1)S(1)}, u32[]{:S(2)}, u32[]{:S(2)}) collective-permute-start(bf16[128,3584]{1,0:T(8,128)(2,1)S(1)} %all_gather.11), channel_id=1, source_target_pairs={{0,8},{8,0},{16,24},{24,16},{1,9},{9,1},{17,25},{25,17},{2,10},{10... | collective-permute-start | bytes 2752520 | tf_op jit(solution)/shard_map/ppermute | solution.py:25
  275.8 93.7 %reduce-scatter.11.cloned.1.call-start = ((), (), s32[]{:S(2)}) async-start(), calls=%async_computation.7 | async-start | bytes 1376256 | tf_op jit(solution)/shard_map/reduce_scatter | solution.py:78
  317.1 14.5 %collective-permute-start.6 = (bf16[2048,128]{1,0:T(8,128)(2,1)}, bf16[2048,128]{1,0:T(8,128)(2,1)}, u32[]{:S(2)}, u32[]{:S(2)}) collective-permute-start(bf16[2048,128]{1,0:T(8,128)(2,1)} %reshape.160), channel_id=1, source_target_pairs={{0,8},{8,16},{16,24},{1,9},{9,17},{17,25},{2,10},{10,18},{18,26},{... | collective-permute-start | bytes 1572872 | tf_op jit(solution)/shard_map/ppermute | solution.py:16
  323.5 15.0 %collective-permute-start.7 = (bf16[2048,128]{1,0:T(8,128)(2,1)}, bf16[2048,128]{1,0:T(8,128)(2,1)}, u32[]{:S(2)}, u32[]{:S(2)}) collective-permute-start(bf16[2048,128]{1,0:T(8,128)(2,1)} %reshape.162), channel_id=1, source_target_pairs={{8,0},{16,8},{24,16},{9,1},{17,9},{25,17},{10,2},{18,10},{26,18},{... | collective-permute-start | bytes 1572872 | tf_op jit(solution)/shard_map/ppermute | solution.py:17
  (1 other events, 3.7 us)
Sparse Core Ops, SparseCore 0:
  15.8 21.6 reduce-scatter.4
  83.8 36.3 all-reduce.6
  186.2 17.8 reduce-scatter.6
  206.1 22.9 reduce-scatter.8
  275.9 36.3 all-reduce.4
  351.4 18.0 reduce-scatter.10
where the time goes:
time: 380 us; the launch traced here: 378 us
  waiting for transfers between devices  142 us (37%)
  matrix products  80.9 us (21%)
  local copies, waits for them, and re-layouts  46.4 us (12%)
  blocking collectives  43.9 us (12%)
  other arithmetic  23.8 us (6%)
  starting transfers between devices  21.1 us (6%)
  between operations  20.1 us (5%)
    psum x2, waiting for transfers between devices, shards(): lax.psum(product.astype(jnp.bfloat16), 'row').astype(jnp.float32)  60.3 us
    dot_general x4, matrix products, shards(): lax.dot_general(hid_operand, weight, (((1,), (1,)), ((), ())), preferred_...  44.9 us
    reduce_scatter x4, waiting for transfers between devices, shards(): lax.psum_scatter(feature_term(jnp.int32(0), col_rows * lax.axis_size('col...  44.3 us
    all_gather x3, blocking collectives, shards(): hid_send = lax.all_gather(hid_share, 'col', axis=0, tiled=True)  43.9 us
    dot_general x4, matrix products, feature_term(): return jnp.dot(operand, weight, preferred_element_type=jnp.float32)  33.8 us
    ppermute x3, waiting for transfers between devices, extended_2(): after = lax.ppermute(first, axis, down)  18.2 us
    ppermute x3, waiting for transfers between devices, swapped(): return lax.ppermute(value, axis, pairs)  16.7 us
    ppermute x3, starting transfers between devices, extended_2(): before = lax.ppermute(last, axis, up)  12.1 us
  transfers between devices with their start and end apart: 15, of which 13 were waited for; matrix products, arithmetic and copies ran while one was open for 20% of the time, Pallas kernels for 0%

commit v1 on v0

--- a/solution.py
+++ b/solution.py
@@ -92,7 +92,9 @@
         )
         updated = (
             residual.astype(jnp.float32)
-            + lax.psum(product.astype(jnp.bfloat16), "row").astype(jnp.float32)
+            + jnp.sum(lax.all_gather(product.astype(jnp.bfloat16), "row"), axis=0).astype(
+                jnp.float32
+            )
         ).astype(jnp.bfloat16)
         fwd_out = jnp.where(is_even, fwd_res, updated)
         bwd_out = jnp.where(is_even, updated, bwd_res)

time: 380 us -> 319 us (0.84)
  local copies, waits for them, and re-layouts: 46.4 us -> 12.7 us
  waiting for transfers between devices: 142 us -> 112 us
  other arithmetic: 23.8 us -> 31.5 us
  blocking collectives: 43.9 us -> 38 us
    psum x2 -> x0, waiting for transfers between devices: 60.3 us -> none  [shards(): lax.psum(product.astype(jnp.bfloat16), 'row').astype(jnp.float32)]
    ppermute x3, waiting for transfers between devices: 16.7 us -> 46.3 us  [swapped(): return lax.ppermute(value, axis, pairs)]
    all_gather x0 -> x4, waiting for transfers between devices: none -> 20.5 us  [shards(): lax.all_gather(product.astype(jnp.bfloat16), 'row')]
    reshape x6 -> x0, local copies, waits for them, and re-layouts: 12.5 us -> none  [the longest x3 6.25 us: shards(): fwd_out.reshape(res_rows, 128)]
    ppermute x3, waiting for transfers between devices: 18.2 us -> 6.77 us  [extended_2(): after = lax.ppermute(first, axis, down)]
    reduce_sum x0 -> x4, other arithmetic: none -> 10.9 us  [shards(): jnp.sum(lax.all_gather(product.astype(jnp.bfloat16), 'row'), axis=0)]
    reduce_scatter x4, waiting for transfers between devices: 44.3 us -> 36.9 us  [shards(): lax.psum_scatter(feature_term(jnp.int32(0), col_rows * lax.axis_size('col...]
    reshape x3 -> x1, local copies, waits for them, and re-layouts: 6.19 us -> 0.22 us  [shards(): left_resid.reshape(fwd_out.shape)]
  transfers between devices with their start and end apart: 15 -> 17, of which waited for: 13 -> 10; matrix products, arithmetic and copies ran while one was open for 20% -> 22% of each run, Pallas kernels for 0% -> 0%
where the time goes in v1:
time: 319 us; the launch traced here: 318 us
  waiting for transfers between devices  112 us (35%)
  matrix products  80.3 us (25%)
  blocking collectives  38 us (12%)
  other arithmetic  31.5 us (10%)
  starting transfers between devices  21.9 us (7%)
  between operations  21.9 us (7%)
  local copies, waits for them, and re-layouts  12.7 us (4%)
    ppermute x3, waiting for transfers between devices, swapped(): return lax.ppermute(value, axis, pairs)  46.3 us
    dot_general x4, matrix products, shards(): lax.dot_general(hid_operand, weight, (((1,), (1,)), ((), ())), preferred_...  45.3 us
    all_gather x3, blocking collectives, shards(): hid_send = lax.all_gather(hid_share, 'col', axis=0, tiled=True)  38 us
    reduce_scatter x4, waiting for transfers between devices, shards(): lax.psum_scatter(feature_term(jnp.int32(0), col_rows * lax.axis_size('col...  36.9 us
    dot_general x4, matrix products, feature_term(): return jnp.dot(operand, weight, preferred_element_type=jnp.float32)  32.8 us
    all_gather x4, waiting for transfers between devices, shards(): lax.all_gather(product.astype(jnp.bfloat16), 'row')  20.5 us
    ppermute x3, starting transfers between devices, extended_2(): before = lax.ppermute(last, axis, up)  12.2 us
    reduce_sum x4, other arithmetic, shards(): jnp.sum(lax.all_gather(product.astype(jnp.bfloat16), 'row'), axis=0)  10.9 us
  transfers between devices with their start and end apart: 17, of which 10 were waited for; matrix products, arithmetic and copies ran while one was open for 22% of the time, Pallas kernels for 0%

profile of v1, /device:TPU:0, one launch (start us, length us, event | category | flops | bytes accessed | tf_op | source)
XLA Modules:
  0.0 317.8 jit_solution(7403859451761201332)
XLA Ops:
  8.1 11.5 %fusion.28 = bf16[128,2048]{1,0:T(8,128)(2,1)} fusion(bf16[1,2048,3584]{2,1,0:T(8,128)(2,1)} %param.13, bf16[1,128,3584]{2,1,0:T(8,128)(2,1)} %param.15, bf16[1,128,3584]{2,1,0:T(8,128)(2,1)} %param.17, bf16[4,1,128,3584]{3,2,1,0:T(8,128)(2,1)} %param.18, pred[]{:T(512)S(6)} %eq.66), kind=kOutput, calls=%fused_computation.20 | convolution fusion | flops 1884815360 | bytes 17956864 | tf_op jit(solution)/shard_map/dot_general | solution.py:90
  19.7 8.2 %fusion.16 = bf16[128,3584]{1,0:T(8,128)(2,1)} fusion(bf16[1,2048,3584]{2,1,0:T(8,128)(2,1)} %param.13, bf16[1,128,2048]{2,1,0:T(8,128)(2,1)S(1)} %copy-done.1, bf16[1,128,2048]{2,1,0:T(8,128)(2,1)S(1)} %copy-done.2, pred[]{:T(512)S(6)} %eq.66), kind=kOutput, calls=%fused_computation.16 | convolution fusion | flops 1879769088 | bytes 16646145 | tf_op jit(solution)/shard_map/dot_general | solution.py:76
  45.3 2.9 reduce_sum.48
  51.9 3.5 %collective-permute-start = (bf16[2048,128]{1,0:T(8,128)(2,1)}, bf16[2048,128]{1,0:T(8,128)(2,1)S(1)}, u32[]{:S(2)}, u32[]{:S(2)}) collective-permute-start(bf16[2048,128]{1,0:T(8,128)(2,1)} %get-tuple-element.12), channel_id=1, source_target_pairs={{0,8},{8,16},{16,24},{1,9},{9,17},{17,25},{2,10},{10,18},{18,26},{... | collective-permute-start | bytes 1572872 | tf_op jit(solution)/shard_map/ppermute | solution.py:16
  58.1 13.1 %all_gather.35 = bf16[128,3584]{1,0:T(8,128)(2,1)} all-gather(bf16[64,3584]{1,0:T(8,128)(2,1)S(1)} %fusion.93), channel_id=1, replica_groups=mesh['pipe'=4,'row'=4,'col'=2] {'col'}, dimensions={0}, use_global_device_ids=true | all-gather | bytes 1376256 | tf_op jit(solution)/shard_map/all_gather | solution.py:102
  76.7 8.2 %fusion.19 = bf16[128,3584]{1,0:T(8,128)(2,1)} fusion(bf16[128,2048]{1,0:T(8,128)(2,1)S(1)} %select_n.273, bf16[1,2048,3584]{2,1,0:T(8,128)(2,1)} %param.13), kind=kOutput, calls=%fused_computation.17 | convolution fusion | flops 1879506944 | bytes 16121856 | tf_op jit(solution)/shard_map/dot_general | solution.py:76
  85.2 8.0 %collective-permute-done.2 = bf16[128,3584]{1,0:T(8,128)(2,1)} collective-permute-done((bf16[128,3584]{1,0:T(8,128)(2,1)}, bf16[128,3584]{1,0:T(8,128)(2,1)}, u32[]{:S(2)}, u32[]{:S(2)}) %collective-permute-start.2) | collective-permute-done | bytes 917536 | tf_op jit(solution)/shard_map/ppermute | solution.py:25
  93.2 11.7 %fusion.31 = bf16[128,2048]{1,0:T(8,128)(2,1)} fusion(bf16[1,2048,3584]{2,1,0:T(8,128)(2,1)} %param.13, bf16[128,3584]{1,0:T(8,128)(2,1)} %collective-permute-done.2, bf16[4,1,128,3584]{3,2,1,0:T(8,128)(2,1)} %param.18, pred[]{:T(512)S(6)} %eq.66), kind=kOutput, calls=%fused_computation.21 | convolution fusion | flops 1884815360 | bytes 17039360 | tf_op jit(solution)/shard_map/dot_general | solution.py:90
  106.3 11.9 %all_gather.38 = bf16[128,3584]{1,0:T(8,128)(2,1)S(1)} all-gather(bf16[64,3584]{1,0:T(8,128)(2,1)S(1)} %fusion.94), channel_id=1, replica_groups=mesh['pipe'=4,'row'=4,'col'=2] {'col'}, dimensions={0}, use_global_device_ids=true | all-gather | bytes 1376256 | tf_op jit(solution)/shard_map/all_gather | solution.py:102
  119.7 18.8 %collective-permute-done.5 = bf16[128,3584]{1,0:T(8,128)(2,1)S(1)} collective-permute-done((bf16[128,3584]{1,0:T(8,128)(2,1)S(1)}, bf16[128,3584]{1,0:T(8,128)(2,1)S(1)}, u32[]{:S(2)}, u32[]{:S(2)}) %collective-permute-start.5) | collective-permute-done | bytes 917536 | tf_op jit(solution)/shard_map/ppermute | solution.py:25
  138.5 11.0 %fusion.34 = bf16[128,2048]{1,0:T(8,128)(2,1)} fusion(bf16[1,2048,3584]{2,1,0:T(8,128)(2,1)} %param.13, bf16[128,3584]{1,0:T(8,128)(2,1)S(1)} %collective-permute-done.5, bf16[4,1,128,3584]{3,2,1,0:T(8,128)(2,1)} %param.18, pred[]{:T(512)S(6)} %eq.66), kind=kOutput, calls=%fused_computation.22 | convolution fusion | flops 1884815360 | bytes 17039360 | tf_op jit(solution)/shard_map/dot_general | solution.py:90
  149.6 3.0 reduce_sum.49
  155.0 4.0 %collective-permute-start.3 = (bf16[2048,128]{1,0:T(8,128)(2,1)}, bf16[2048,128]{1,0:T(8,128)(2,1)}, u32[]{:S(2)}, u32[]{:S(2)}) collective-permute-start(bf16[2048,128]{1,0:T(8,128)(2,1)} %get-tuple-element.10), channel_id=1, source_target_pairs={{0,8},{8,16},{16,24},{1,9},{9,17},{17,25},{2,10},{10,18},{18,26},{... | collective-permute-start | bytes 1572872 | tf_op jit(solution)/shard_map/ppermute | solution.py:16
  161.7 10.6 %all-gather.13.cloned.1.call-done = bf16[512,2048]{1,0:T(8,128)(2,1)} async-done(((bf16[128,2048]{1,0:T(8,128)(2,1)}), bf16[512,2048]{1,0:T(8,128)(2,1)}) %all-gather.13.cloned.1.call-update) | async-done | bytes 2097168 | tf_op jit(solution)/shard_map/all_gather | solution.py:95
  177.3 8.2 %fusion.22 = bf16[128,3584]{1,0:T(8,128)(2,1)} fusion(bf16[128,2048]{1,0:T(8,128)(2,1)S(1)} %select_n.283, bf16[1,2048,3584]{2,1,0:T(8,128)(2,1)} %param.13), kind=kOutput, calls=%fused_computation.18 | convolution fusion | flops 1879506944 | bytes 16121856 | tf_op jit(solution)/shard_map/dot_general | solution.py:76
  185.5 19.0 %reduce-scatter.9.cloned.1.call-done = bf16[64,3584]{1,0:T(8,128)(2,1)} async-done(((bf16[128,3584]{1,0:T(8,128)(2,1)}), bf16[64,3584]{1,0:T(8,128)(2,1)}) %reduce-scatter.9.cloned.1.call-update) | async-done | bytes 458768 | tf_op jit(solution)/shard_map/reduce_scatter | solution.py:78
  205.7 12.9 %all_gather.41 = bf16[128,3584]{1,0:T(8,128)(2,1)S(1)} all-gather(bf16[64,3584]{1,0:T(8,128)(2,1)S(1)} %fusion.95), channel_id=1, replica_groups=mesh['pipe'=4,'row'=4,'col'=2] {'col'}, dimensions={0}, use_global_device_ids=true | all-gather | bytes 1376256 | tf_op jit(solution)/shard_map/all_gather | solution.py:102
  220.1 19.5 %collective-permute-done.8 = bf16[128,3584]{1,0:T(8,128)(2,1)S(1)} collective-permute-done((bf16[128,3584]{1,0:T(8,128)(2,1)S(1)}, bf16[128,3584]{1,0:T(8,128)(2,1)S(1)}, u32[]{:S(2)}, u32[]{:S(2)}) %collective-permute-start.8) | collective-permute-done | bytes 917536 | tf_op jit(solution)/shard_map/ppermute | solution.py:25
  239.7 11.0 %fusion.37 = bf16[128,2048]{1,0:T(8,128)(2,1)} fusion(bf16[1,2048,3584]{2,1,0:T(8,128)(2,1)} %param.13, bf16[128,3584]{1,0:T(8,128)(2,1)S(1)} %collective-permute-done.8, bf16[4,1,128,3584]{3,2,1,0:T(8,128)(2,1)} %param.18, pred[]{:T(512)S(6)} %eq.66), kind=kOutput, calls=%fused_computation.23 | convolution fusion | flops 1884815360 | bytes 17039360 | tf_op jit(solution)/shard_map/dot_general | solution.py:90
  252.1 4.6 %collective-permute-start.6 = (bf16[2048,128]{1,0:T(8,128)(2,1)S(1)}, bf16[2048,128]{1,0:T(8,128)(2,1)S(1)}, u32[]{:S(2)}, u32[]{:S(2)}) collective-permute-start(bf16[2048,128]{1,0:T(8,128)(2,1)S(1)} %copy-done.11), channel_id=1, source_target_pairs={{0,8},{8,16},{16,24},{1,9},{9,17},{17,25},{2,10},{10,18},{18,26},{... | collective-permute-start | bytes 1572872 | tf_op jit(solution)/shard_map/ppermute | solution.py:16
  257.6 6.8 %collective-permute-done.7 = bf16[2048,128]{1,0:T(8,128)(2,1)S(1)} collective-permute-done((bf16[2048,128]{1,0:T(8,128)(2,1)S(1)}, bf16[2048,128]{1,0:T(8,128)(2,1)S(1)}, u32[]{:S(2)}, u32[]{:S(2)}) %collective-permute-start.7) | collective-permute-done | bytes 524320 | tf_op jit(solution)/shard_map/ppermute | solution.py:17
  265.8 7.6 %all-gather.15.cloned.1.call-done = bf16[512,2048]{1,0:T(8,128)(2,1)} async-done(((bf16[128,2048]{1,0:T(8,128)(2,1)}), bf16[512,2048]{1,0:T(8,128)(2,1)}) %all-gather.15.cloned.1.call-update) | async-done | bytes 2097168 | tf_op jit(solution)/shard_map/all_gather | solution.py:95
  281.2 8.3 %fusion.25 = bf16[128,3584]{1,0:T(8,128)(2,1)} fusion(bf16[128,2048]{1,0:T(8,128)(2,1)S(1)} %select_n.292, bf16[1,2048,3584]{2,1,0:T(8,128)(2,1)} %param.13), kind=kOutput, calls=%fused_computation.19 | convolution fusion | flops 1879506944 | bytes 16121856 | tf_op jit(solution)/shard_map/dot_general | solution.py:76
  290.5 17.9 %reduce-scatter.11.cloned.1.call-done = bf16[64,3584]{1,0:T(8,128)(2,1)} async-done(((bf16[128,3584]{1,0:T(8,128)(2,1)}), bf16[64,3584]{1,0:T(8,128)(2,1)}) %reduce-scatter.11.cloned.1.call-update) | async-done | bytes 458768 | tf_op jit(solution)/shard_map/reduce_scatter | solution.py:78
  (108 shorter events, 53.6 us)
Async XLA Ops:
  8.0 34.4 %copy-start = (bf16[8,2048]{1,0:T(8,128)(2,1)S(1)}, bf16[8,2048]{1,0:T(8,128)(2,1)}, u32[]{:S(2)}) copy-start(bf16[8,2048]{1,0:T(8,128)(2,1)} %param.24) | copy-start | bytes 98308
  8.0 37.3 %all-gather.9.cloned.1.call-start = ((), (), s32[]{:S(2)}) async-start(), calls=%async_computation.8 | async-start | bytes 2621440 | tf_op jit(solution)/shard_map/all_gather | solution.py:95
  8.1 11.6 %copy-start.1 = (bf16[1,128,2048]{2,1,0:T(8,128)(2,1)S(1)}, bf16[1,128,2048]{2,1,0:T(8,128)(2,1)}, u32[]{:S(2)}) copy-start(bf16[1,128,2048]{2,1,0:T(8,128)(2,1)} %param.14) | copy-start | bytes 1572868
  8.1 11.6 %copy-start.2 = (bf16[1,128,2048]{2,1,0:T(8,128)(2,1)S(1)}, bf16[1,128,2048]{2,1,0:T(8,128)(2,1)}, u32[]{:S(2)}) copy-start(bf16[1,128,2048]{2,1,0:T(8,128)(2,1)} %param.16) | copy-start | bytes 1572868
  19.6 37.2 %reduce-scatter.5.cloned.1.call-start = ((), (), s32[]{:S(2)}) async-start(), calls=%async_computation.4 | async-start | bytes 1376256 | tf_op jit(solution)/shard_map/reduce_scatter | solution.py:78
  27.9 77.1 %reduce-scatter.7.cloned.1.call-start = ((), (), s32[]{:S(2)}) async-start(), calls=%async_computation.5 | async-start | bytes 1376256 | tf_op jit(solution)/shard_map/reduce_scatter | solution.py:78
  51.9 22.4 %copy-start.3 = (bf16[2048,128]{1,0:T(8,128)(2,1)S(1)}, bf16[2048,128]{1,0:T(8,128)(2,1)}, u32[]{:S(2)}) copy-start(bf16[2048,128]{1,0:T(8,128)(2,1)} %squeeze.54) | copy-start | bytes 1572868
  51.9 21.7 %collective-permute-start = (bf16[2048,128]{1,0:T(8,128)(2,1)}, bf16[2048,128]{1,0:T(8,128)(2,1)S(1)}, u32[]{:S(2)}, u32[]{:S(2)}) collective-permute-start(bf16[2048,128]{1,0:T(8,128)(2,1)} %get-tuple-element.12), channel_id=1, source_target_pairs={{0,8},{8,16},{16,24},{1,9},{9,17},{17,25},{2,10},{10,18},{18,26},{... | collective-permute-start | bytes 1572872 | tf_op jit(solution)/shard_map/ppermute | solution.py:16
  55.5 18.1 %collective-permute-start.1 = (bf16[2048,128]{1,0:T(8,128)(2,1)}, bf16[2048,128]{1,0:T(8,128)(2,1)}, u32[]{:S(2)}, u32[]{:S(2)}) collective-permute-start(bf16[2048,128]{1,0:T(8,128)(2,1)} %get-tuple-element.13), channel_id=1, source_target_pairs={{8,0},{16,8},{24,16},{9,1},{17,9},{25,17},{10,2},{18,10},{26,18},{... | collective-permute-start | bytes 1572872 | tf_op jit(solution)/shard_map/ppermute | solution.py:17
  71.2 22.0 %collective-permute-start.2 = (bf16[128,3584]{1,0:T(8,128)(2,1)}, bf16[128,3584]{1,0:T(8,128)(2,1)}, u32[]{:S(2)}, u32[]{:S(2)}) collective-permute-start(bf16[128,3584]{1,0:T(8,128)(2,1)} %all_gather.35), channel_id=1, source_target_pairs={{0,8},{8,0},{16,24},{24,16},{1,9},{9,1},{17,25},{25,17},{2,10},{10... | collective-permute-start | bytes 2752520 | tf_op jit(solution)/shard_map/ppermute | solution.py:25
  84.9 64.6 %all-gather.11.cloned.1.call-start = ((), (), s32[]{:S(2)}) async-start(), calls=%async_computation.9 | async-start | bytes 2621440 | tf_op jit(solution)/shard_map/all_gather | solution.py:95
  104.9 67.4 %all-gather.13.cloned.1.call-start = ((), (), s32[]{:S(2)}) async-start(), calls=%async_computation.10 | async-start | bytes 2621440 | tf_op jit(solution)/shard_map/all_gather | solution.py:95
  118.2 20.2 %collective-permute-start.5 = (bf16[128,3584]{1,0:T(8,128)(2,1)S(1)}, bf16[128,3584]{1,0:T(8,128)(2,1)S(1)}, u32[]{:S(2)}, u32[]{:S(2)}) collective-permute-start(bf16[128,3584]{1,0:T(8,128)(2,1)S(1)} %all_gather.38), channel_id=1, source_target_pairs={{0,8},{8,0},{16,24},{24,16},{1,9},{9,1},{17,25},{25,17},{2,10},{10... | collective-permute-start | bytes 2752520 | tf_op jit(solution)/shard_map/ppermute | solution.py:25
  149.5 54.9 %reduce-scatter.9.cloned.1.call-start = ((), (), s32[]{:S(2)}) async-start(), calls=%async_computation.6 | async-start | bytes 1376256 | tf_op jit(solution)/shard_map/reduce_scatter | solution.py:78
  155.0 19.6 %collective-permute-start.3 = (bf16[2048,128]{1,0:T(8,128)(2,1)}, bf16[2048,128]{1,0:T(8,128)(2,1)}, u32[]{:S(2)}, u32[]{:S(2)}) collective-permute-start(bf16[2048,128]{1,0:T(8,128)(2,1)} %get-tuple-element.10), channel_id=1, source_target_pairs={{0,8},{8,16},{16,24},{1,9},{9,17},{17,25},{2,10},{10,18},{18,26},{... | collective-permute-start | bytes 1572872 | tf_op jit(solution)/shard_map/ppermute | solution.py:16
  159.1 15.5 %collective-permute-start.4 = (bf16[2048,128]{1,0:T(8,128)(2,1)}, bf16[2048,128]{1,0:T(8,128)(2,1)}, u32[]{:S(2)}, u32[]{:S(2)}) collective-permute-start(bf16[2048,128]{1,0:T(8,128)(2,1)} %get-tuple-element.11), channel_id=1, source_target_pairs={{8,0},{16,8},{24,16},{9,1},{17,9},{25,17},{10,2},{18,10},{26,18},{... | collective-permute-start | bytes 1572872 | tf_op jit(solution)/shard_map/ppermute | solution.py:17
  185.5 88.0 %all-gather.15.cloned.1.call-start = ((), (), s32[]{:S(2)}) async-start(), calls=%async_computation.11 | async-start | bytes 2621440 | tf_op jit(solution)/shard_map/all_gather | solution.py:95
  218.7 33.4 %copy-start.11 = (bf16[2048,128]{1,0:T(8,128)(2,1)S(1)}, bf16[2048,128]{1,0:T(8,128)(2,1)}, u32[]{:S(2)}) copy-start(bf16[2048,128]{1,0:T(8,128)(2,1)} %get-tuple-element.2) | copy-start | bytes 1572868
  218.7 21.0 %collective-permute-start.8 = (bf16[128,3584]{1,0:T(8,128)(2,1)S(1)}, bf16[128,3584]{1,0:T(8,128)(2,1)S(1)}, u32[]{:S(2)}, u32[]{:S(2)}) collective-permute-start(bf16[128,3584]{1,0:T(8,128)(2,1)S(1)} %all_gather.41), channel_id=1, source_target_pairs={{0,8},{8,0},{16,24},{24,16},{1,9},{9,1},{17,25},{25,17},{2,10},{10... | collective-permute-start | bytes 2752520 | tf_op jit(solution)/shard_map/ppermute | solution.py:25
  250.7 57.7 %reduce-scatter.11.cloned.1.call-start = ((), (), s32[]{:S(2)}) async-start(), calls=%async_computation.7 | async-start | bytes 1376256 | tf_op jit(solution)/shard_map/reduce_scatter | solution.py:78
  250.8 13.6 %collective-permute-start.7 = (bf16[2048,128]{1,0:T(8,128)(2,1)S(1)}, bf16[2048,128]{1,0:T(8,128)(2,1)S(1)}, u32[]{:S(2)}, u32[]{:S(2)}) collective-permute-start(bf16[2048,128]{1,0:T(8,128)(2,1)S(1)} %get-tuple-element.20), channel_id=1, source_target_pairs={{8,0},{16,8},{24,16},{9,1},{17,9},{25,17},{10,2},{18,10},{26,18},{... | collective-permute-start | bytes 1572872 | tf_op jit(solution)/shard_map/ppermute | solution.py:17
  252.1 13.5 %collective-permute-start.6 = (bf16[2048,128]{1,0:T(8,128)(2,1)S(1)}, bf16[2048,128]{1,0:T(8,128)(2,1)S(1)}, u32[]{:S(2)}, u32[]{:S(2)}) collective-permute-start(bf16[2048,128]{1,0:T(8,128)(2,1)S(1)} %copy-done.11), channel_id=1, source_target_pairs={{0,8},{8,16},{16,24},{1,9},{9,17},{17,25},{2,10},{10,18},{18,26},{... | collective-permute-start | bytes 1572872 | tf_op jit(solution)/shard_map/ppermute | solution.py:16
  264.4 11.9 %copy-start.8 = (bf16[2048,128]{1,0:T(8,128)(2,1)}, bf16[2048,128]{1,0:T(8,128)(2,1)S(1)}, u32[]{:S(2)}) copy-start(bf16[2048,128]{1,0:T(8,128)(2,1)S(1)} %collective-permute-done.7) | copy-start | bytes 1572868
  265.6 10.8 %copy-start.9 = (bf16[2048,128]{1,0:T(8,128)(2,1)}, bf16[2048,128]{1,0:T(8,128)(2,1)S(1)}, u32[]{:S(2)}) copy-start(bf16[2048,128]{1,0:T(8,128)(2,1)S(1)} %collective-permute-done.6) | copy-start | bytes 1572868
  (9 other events, 41.4 us)
Sparse Core Ops, SparseCore 0:
  19.7 25.5 all-gather.8
  105.1 23.6 all-gather.10
  149.6 22.6 all-gather.12
  250.8 22.5 all-gather.14
Sparse Core Ops, SparseCore 1:
  28.0 21.9 reduce-scatter.4
  85.0 19.2 reduce-scatter.6
  185.5 18.9 reduce-scatter.8
  289.5 18.8 reduce-scatter.10
